TPU v7x, 32 devices: a whole 2x2x4 slice. The times are simulated.
32 devices in a mesh: dp: 32 (over z, y, x, core).
Axes of the slice: x: 2, y: 2, z: 4, core: 2. Of those that a mesh axis runs over, the one named last changes fastest.
Arguments:
- points: float32 [16384, 17], P('dp')
- targets: float32 [16384], P('dp')
- probes: float32 [16384, 16], P('dp')
- log_l: float32 [], replicated
- log_s: float32 [], replicated
- log_sigma: float32 [], replicated
Outputs:
- output 1: float32 [16384], P('dp')
- output 2: float32 [16384, 16], P('dp')
- output 3: float32 [4], replicated
All inputs are finite; a program needn't handle non-finite values.
Results may differ from a plain program's by a relative error of at most 0.001.
Values sent between devices are 32-bit elements.
A program may use at most 1 GiB of HBM per device.

v0:
```python
import jax
import jax.numpy as jnp
from jax import lax
from jax.sharding import PartitionSpec as P

CG_STEPS = 20


def tile_sums(row_points, row_sq, points, sq_norms, right, inv_two_l2, with_dist):
    n_total = points.shape[0]
    col_tile = min(n_total, 1024)
    zeros = jnp.zeros((row_points.shape[0], right.shape[1]), jnp.float32)
    start_totals = (zeros, zeros) if with_dist else (zeros,)

    def body(index, totals):
        start = index * col_tile
        col_points = lax.dynamic_slice_in_dim(points, start, col_tile)
        col_sq = lax.dynamic_slice_in_dim(sq_norms, start, col_tile)
        col_right = lax.dynamic_slice_in_dim(right, start, col_tile)
        cross = lax.dot_general(row_points, col_points, (((1,), (1,)), ((), ())), precision=lax.Precision.HIGHEST, preferred_element_type=jnp.float32)
        dist_sq = jnp.maximum(row_sq[:, None] + col_sq[None, :] - 2.0 * cross, 0.0)
        kernel = jnp.exp(-dist_sq * inv_two_l2)
        first = totals[0] + jnp.dot(kernel, col_right, precision=lax.Precision.HIGHEST, preferred_element_type=jnp.float32)
        if with_dist:
            second = totals[1] + jnp.dot(kernel * dist_sq, col_right, precision=lax.Precision.HIGHEST, preferred_element_type=jnp.float32)
            return (first, second)
        return (first,)

    return lax.fori_loop(0, n_total // col_tile, body, start_totals)


def solution(mesh):
    def local(points_own, targets_own, probes_own, log_l, log_s, log_sigma):
        probe_count = probes_own.shape[1]
        inv_two_l2 = 0.5 * jnp.exp(-2.0 * log_l)
        out_var = jnp.exp(2.0 * log_s)
        noise_var = jnp.exp(2.0 * log_sigma)
        sq_own = jnp.sum(points_own * points_own, axis=1)

        def gather_points():
            points_all = lax.all_gather(points_own, "dp", tiled=True)
            return points_all, jnp.sum(points_all * points_all, axis=1)

        def apply_kernel(search_own):
            points_all, sq_all = gather_points()
            search_all = lax.all_gather(search_own, "dp", tiled=True)
            totals = tile_sums(points_own, sq_own, points_all, sq_all, search_all, inv_two_l2, False)
            return out_var * totals[0] + noise_var * search_own

        right_sides = jnp.concatenate([targets_own[:, None], probes_own], axis=1)
        solved = jnp.zeros_like(right_sides)
        residual = right_sides
        search = right_sides
        res_norm = lax.psum(jnp.sum(right_sides * right_sides, axis=0), "dp")
        for step in range(CG_STEPS):
            product = apply_kernel(search)
            alpha = res_norm / lax.psum(jnp.sum(search * product, axis=0), "dp")
            solved = solved + alpha * search
            if step < CG_STEPS - 1:
                residual = residual - alpha * product
                new_norm = lax.psum(jnp.sum(residual * residual, axis=0), "dp")
                search = residual + (new_norm / res_norm) * search
                res_norm = new_norm

        u_own = solved[:, 0]
        v_own = solved[:, 1:]
        left = jnp.concatenate([u_own[:, None], -v_own / probe_count], axis=1)
        right_own = jnp.concatenate([u_own[:, None], probes_own], axis=1)
        points_all, sq_all = gather_points()
        right_all = lax.all_gather(right_own, "dp", tiled=True)
        kern_right, dist_right = tile_sums(points_own, sq_own, points_all, sq_all, right_all, inv_two_l2, True)
        n_total = points_all.shape[0]
        local_sums = jnp.stack([
            out_var * inv_two_l2 * jnp.sum(left * dist_right),
            out_var * jnp.sum(left * kern_right),
            noise_var * jnp.sum(left * right_own),
            0.5 * jnp.sum(targets_own * u_own),
        ]) / n_total
        return u_own, v_own, lax.psum(local_sums, "dp")

    return jax.shard_map(
        local,
        mesh=mesh,
        in_specs=(P("dp", None), P("dp"), P("dp", None), P(), P(), P()),
        out_specs=(P("dp"), P("dp", None), P()),
        check_vma=False,
    )
```

profile of v0, /device:TPU:0, one launch (start us, length us, event | category | flops | bytes accessed | tf_op | source)
XLA Modules:
  0.0 4922.7 jit_solution(14140579556861555645)
XLA Ops:
  12.3 56.1 %all-gather.23.cloned.1.call-done = f32[16384,17]{0,1:T(8,128)} async-done(((f32[512,17]{0,1:T(8,128)}), f32[16384,17]{0,1:T(8,128)}) %all-gather.23.cloned.1.call-update) | async-done | bytes 1114128 | tf_op jit(solution)/shard_map/all_gather | solution.py:41
  70.0 54.9 %all-gather.25.cloned.1.call-done = f32[16384,17]{0,1:T(8,128)} async-done(((f32[512,17]{0,1:T(8,128)}), f32[16384,17]{0,1:T(8,128)}) %all-gather.25.cloned.1.call-update) | async-done | bytes 1114128 | tf_op jit(solution)/shard_map/all_gather | solution.py:46
  124.9 98.5 %while.296 = (s32[]{:T(128)}, f32[512,17]{0,1:T(8,128)S(1)}, f32[512]{0:T(512)S(1)}, f32[16384]{0:T(1024)S(1)}, f32[16384,17]{0,1:T(8,128)}, /*index=5*/f32[512,...) while((s32[]{:T(128)}, f32[512,17]{0,1:T(8,128)S(1)}, ...), condition=%wide.region_5.0_spmd.clone, body=%wide.region_4.0_spmd.clone.sunk | while | flops 217072640 | bytes 4524729 | solution.py:29
  303.6 54.5 %all-gather.27.cloned.1.call-done = f32[16384,17]{0,1:T(8,128)} async-done(((f32[512,17]{0,1:T(8,128)}), f32[16384,17]{0,1:T(8,128)}) %all-gather.27.cloned.1.call-update) | async-done | bytes 1114128 | tf_op jit(solution)/shard_map/all_gather | solution.py:46
  358.1 98.5 %while.297 = (s32[]{:T(128)}, f32[512,17]{0,1:T(8,128)S(1)}, f32[512]{0:T(512)S(1)}, f32[16384]{0:T(1024)S(1)}, f32[16384,17]{0,1:T(8,128)}, /*index=5*/f32[512,...) while((s32[]{:T(128)}, f32[512,17]{0,1:T(8,128)S(1)}, ...), condition=%wide.region_11.0_spmd.clone, body=%wide.region_10.0_spmd.clone.sunk | while | flops 217072640 | bytes 4524729 | solution.py:29
  591.2 98.4 %while.298 = (s32[]{:T(128)}, f32[512,17]{0,1:T(8,128)S(1)}, f32[512]{0:T(512)S(1)}, f32[16384]{0:T(1024)S(1)}, f32[16384,17]{0,1:T(8,128)}, /*index=5*/f32[512,...) while((s32[]{:T(128)}, f32[512,17]{0,1:T(8,128)S(1)}, ...), condition=%wide.region_17.0_spmd.clone, body=%wide.region_16.0_spmd.clone.sunk | while | flops 217072640 | bytes 4524729 | solution.py:29
  769.9 54.5 %all-gather.31.cloned.1.call-done = f32[16384,17]{0,1:T(8,128)} async-done(((f32[512,17]{0,1:T(8,128)}), f32[16384,17]{0,1:T(8,128)}) %all-gather.31.cloned.1.call-update) | async-done | bytes 1114128 | tf_op jit(solution)/shard_map/all_gather | solution.py:46
  824.4 98.5 %while.299 = (s32[]{:T(128)}, f32[512,17]{0,1:T(8,128)S(1)}, f32[512]{0:T(512)S(1)}, f32[16384]{0:T(1024)S(1)}, f32[16384,17]{0,1:T(8,128)}, /*index=5*/f32[512,...) while((s32[]{:T(128)}, f32[512,17]{0,1:T(8,128)S(1)}, ...), condition=%wide.region_23.0_spmd.clone, body=%wide.region_22.0_spmd.clone.sunk | while | flops 217072640 | bytes 4524729 | solution.py:29
  1057.6 98.4 %while.300 = (s32[]{:T(128)}, f32[512,17]{0,1:T(8,128)S(1)}, f32[512]{0:T(512)S(1)}, f32[16384]{0:T(1024)S(1)}, f32[16384,17]{0,1:T(8,128)}, /*index=5*/f32[512,...) while((s32[]{:T(128)}, f32[512,17]{0,1:T(8,128)S(1)}, ...), condition=%wide.region_29.0_spmd.clone, body=%wide.region_28.0_spmd.clone.sunk | while | flops 217072640 | bytes 4524729 | solution.py:29
  1236.2 54.5 %all-gather.35.cloned.1.call-done = f32[16384,17]{0,1:T(8,128)} async-done(((f32[512,17]{0,1:T(8,128)}), f32[16384,17]{0,1:T(8,128)}) %all-gather.35.cloned.1.call-update) | async-done | bytes 1114128 | tf_op jit(solution)/shard_map/all_gather | solution.py:46
  1290.7 98.4 %while.301 = (s32[]{:T(128)}, f32[512,17]{0,1:T(8,128)S(1)}, f32[512]{0:T(512)S(1)}, f32[16384]{0:T(1024)S(1)}, f32[16384,17]{0,1:T(8,128)}, /*index=5*/f32[512,...) while((s32[]{:T(128)}, f32[512,17]{0,1:T(8,128)S(1)}, ...), condition=%wide.region_35.0_spmd.clone, body=%wide.region_34.0_spmd.clone.sunk | while | flops 217072640 | bytes 4524729 | solution.py:29
  1523.8 98.4 %while.302 = (s32[]{:T(128)}, f32[512,17]{0,1:T(8,128)S(1)}, f32[512]{0:T(512)S(1)}, f32[16384]{0:T(1024)S(1)}, f32[16384,17]{0,1:T(8,128)}, /*index=5*/f32[512,...) while((s32[]{:T(128)}, f32[512,17]{0,1:T(8,128)S(1)}, ...), condition=%wide.region_41.0_spmd.clone, body=%wide.region_40.0_spmd.clone.sunk | while | flops 217072640 | bytes 4524729 | solution.py:29
  1702.5 54.5 %all-gather.39.cloned.1.call-done = f32[16384,17]{0,1:T(8,128)} async-done(((f32[512,17]{0,1:T(8,128)}), f32[16384,17]{0,1:T(8,128)}) %all-gather.39.cloned.1.call-update) | async-done | bytes 1114128 | tf_op jit(solution)/shard_map/all_gather | solution.py:46
  1757.0 98.5 %while.303 = (s32[]{:T(128)}, f32[512,17]{0,1:T(8,128)S(1)}, f32[512]{0:T(512)S(1)}, f32[16384]{0:T(1024)S(1)}, f32[16384,17]{0,1:T(8,128)}, /*index=5*/f32[512,...) while((s32[]{:T(128)}, f32[512,17]{0,1:T(8,128)S(1)}, ...), condition=%wide.region_47.0_spmd.clone, body=%wide.region_46.0_spmd.clone.sunk | while | flops 217072640 | bytes 4524729 | solution.py:29
  1990.2 98.4 %while.304 = (s32[]{:T(128)}, f32[512,17]{0,1:T(8,128)S(1)}, f32[512]{0:T(512)S(1)}, f32[16384]{0:T(1024)S(1)}, f32[16384,17]{0,1:T(8,128)}, /*index=5*/f32[512,...) while((s32[]{:T(128)}, f32[512,17]{0,1:T(8,128)S(1)}, ...), condition=%wide.region_53.0_spmd.clone, body=%wide.region_52.0_spmd.clone.sunk | while | flops 217072640 | bytes 4524729 | solution.py:29
  2168.8 54.5 %all-gather.43.cloned.1.call-done = f32[16384,17]{0,1:T(8,128)} async-done(((f32[512,17]{0,1:T(8,128)}), f32[16384,17]{0,1:T(8,128)}) %all-gather.43.cloned.1.call-update) | async-done | bytes 1114128 | tf_op jit(solution)/shard_map/all_gather | solution.py:46
  2223.3 98.4 %while.305 = (s32[]{:T(128)}, f32[512,17]{0,1:T(8,128)S(1)}, f32[512]{0:T(512)S(1)}, f32[16384]{0:T(1024)S(1)}, f32[16384,17]{0,1:T(8,128)}, /*index=5*/f32[512,...) while((s32[]{:T(128)}, f32[512,17]{0,1:T(8,128)S(1)}, ...), condition=%wide.region_59.0_spmd.clone, body=%wide.region_58.0_spmd.clone.sunk | while | flops 217072640 | bytes 4524729 | solution.py:29
  2456.5 98.4 %while.306 = (s32[]{:T(128)}, f32[512,17]{0,1:T(8,128)S(1)}, f32[512]{0:T(512)S(1)}, f32[16384]{0:T(1024)S(1)}, f32[16384,17]{0,1:T(8,128)}, /*index=5*/f32[512,...) while((s32[]{:T(128)}, f32[512,17]{0,1:T(8,128)S(1)}, ...), condition=%wide.region_65.0_spmd.clone, body=%wide.region_64.0_spmd.clone.sunk | while | flops 217072640 | bytes 4524729 | solution.py:29
  2635.1 54.5 %all-gather.47.cloned.1.call-done = f32[16384,17]{0,1:T(8,128)} async-done(((f32[512,17]{0,1:T(8,128)}), f32[16384,17]{0,1:T(8,128)}) %all-gather.47.cloned.1.call-update) | async-done | bytes 1114128 | tf_op jit(solution)/shard_map/all_gather | solution.py:46
  2689.6 98.5 %while.307 = (s32[]{:T(128)}, f32[512,17]{0,1:T(8,128)S(1)}, f32[512]{0:T(512)S(1)}, f32[16384]{0:T(1024)S(1)}, f32[16384,17]{0,1:T(8,128)}, /*index=5*/f32[512,...) while((s32[]{:T(128)}, f32[512,17]{0,1:T(8,128)S(1)}, ...), condition=%wide.region_71.0_spmd.clone, body=%wide.region_70.0_spmd.clone.sunk | while | flops 217072640 | bytes 4524729 | solution.py:29
  2922.8 98.4 %while.308 = (s32[]{:T(128)}, f32[512,17]{0,1:T(8,128)S(1)}, f32[512]{0:T(512)S(1)}, f32[16384]{0:T(1024)S(1)}, f32[16384,17]{0,1:T(8,128)}, /*index=5*/f32[512,...) while((s32[]{:T(128)}, f32[512,17]{0,1:T(8,128)S(1)}, ...), condition=%wide.region_77.0_spmd.clone, body=%wide.region_76.0_spmd.clone.sunk | while | flops 217072640 | bytes 4524729 | solution.py:29
  3155.9 98.4 %while.309 = (s32[]{:T(128)}, f32[512,17]{0,1:T(8,128)S(1)}, f32[512]{0:T(512)S(1)}, f32[16384]{0:T(1024)S(1)}, f32[16384,17]{0,1:T(8,128)}, /*index=5*/f32[512,...) while((s32[]{:T(128)}, f32[512,17]{0,1:T(8,128)S(1)}, ...), condition=%wide.region_83.0_spmd.clone, body=%wide.region_82.0_spmd.clone.sunk | while | flops 217072640 | bytes 4524729 | solution.py:29
  3389.1 98.4 %while.310 = (s32[]{:T(128)}, f32[512,17]{0,1:T(8,128)S(1)}, f32[512]{0:T(512)S(1)}, f32[16384]{0:T(1024)S(1)}, f32[16384,17]{0,1:T(8,128)}, /*index=5*/f32[512,...) while((s32[]{:T(128)}, f32[512,17]{0,1:T(8,128)S(1)}, ...), condition=%wide.region_89.0_spmd.clone, body=%wide.region_88.0_spmd.clone.sunk | while | flops 217072640 | bytes 4524729 | solution.py:29
  3567.7 54.5 %all-gather.55.cloned.1.call-done = f32[16384,17]{0,1:T(8,128)} async-done(((f32[512,17]{0,1:T(8,128)}), f32[16384,17]{0,1:T(8,128)}) %all-gather.55.cloned.1.call-update) | async-done | bytes 1114128 | tf_op jit(solution)/shard_map/all_gather | solution.py:46
  3622.2 98.5 %while.311 = (s32[]{:T(128)}, f32[512,17]{0,1:T(8,128)S(1)}, f32[512]{0:T(512)S(1)}, f32[16384]{0:T(1024)S(1)}, f32[16384,17]{0,1:T(8,128)}, /*index=5*/f32[512,...) while((s32[]{:T(128)}, f32[512,17]{0,1:T(8,128)S(1)}, ...), condition=%wide.region_95.0_spmd.clone, body=%wide.region_94.0_spmd.clone.sunk | while | flops 217072640 | bytes 4524729 | solution.py:29
  3855.4 98.4 %while.312 = (s32[]{:T(128)}, f32[512,17]{0,1:T(8,128)S(1)}, f32[512]{0:T(512)S(1)}, f32[16384]{0:T(1024)S(1)}, f32[16384,17]{0,1:T(8,128)}, /*index=5*/f32[512,...) while((s32[]{:T(128)}, f32[512,17]{0,1:T(8,128)S(1)}, ...), condition=%wide.region_101.0_spmd.clone, body=%wide.region_100.0_spmd.clone.sunk | while | flops 217072640 | bytes 4524729 | solution.py:29
  4034.1 54.5 %all-gather.59.cloned.1.call-done = f32[16384,17]{0,1:T(8,128)} async-done(((f32[512,17]{0,1:T(8,128)}), f32[16384,17]{0,1:T(8,128)}) %all-gather.59.cloned.1.call-update) | async-done | bytes 1114128 | tf_op jit(solution)/shard_map/all_gather | solution.py:46
  4088.6 98.5 %while.313 = (s32[]{:T(128)}, f32[512,17]{0,1:T(8,128)S(1)}, f32[512]{0:T(512)S(1)}, f32[16384]{0:T(1024)S(1)}, f32[16384,17]{0,1:T(8,128)}, /*index=5*/f32[512,...) while((s32[]{:T(128)}, f32[512,17]{0,1:T(8,128)S(1)}, ...), condition=%wide.region_107.0_spmd.clone, body=%wide.region_106.0_spmd.clone.sunk | while | flops 217072640 | bytes 4524729 | solution.py:29
  4321.8 98.5 %while.314 = (s32[]{:T(128)}, f32[512,17]{0,1:T(8,128)S(1)}, f32[512]{0:T(512)S(1)}, f32[16384]{0:T(1024)S(1)}, f32[16384,17]{0,1:T(8,128)}, /*index=5*/f32[512,...) while((s32[]{:T(128)}, f32[512,17]{0,1:T(8,128)S(1)}, ...), condition=%wide.region_113.0_spmd.clone, body=%wide.region_112.0_spmd.clone.sunk | while | flops 217072640 | bytes 4524729 | solution.py:29
  4500.5 54.5 %all-gather.63.cloned.1.call-done = f32[16384,17]{0,1:T(8,128)} async-done(((f32[512,17]{0,1:T(8,128)}), f32[16384,17]{0,1:T(8,128)}) %all-gather.63.cloned.1.call-update) | async-done | bytes 1114128 | tf_op jit(solution)/shard_map/all_gather | solution.py:46
  4555.0 98.6 %while.315 = (s32[]{:T(128)}, f32[512,17]{0,1:T(8,128)S(1)}, f32[512]{0:T(512)S(1)}, f32[16384]{0:T(1024)S(1)}, f32[16384,17]{0,1:T(8,128)}, /*index=5*/f32[512,...) while((s32[]{:T(128)}, f32[512,17]{0,1:T(8,128)S(1)}, ...), condition=%wide.region_119.0_spmd.clone, body=%wide.region_118.0_spmd.clone.sunk | while | flops 217072640 | bytes 4524729 | solution.py:29
  4748.6 124.9 %while.316 = (s32[]{:T(128)}, f32[512,17]{0,1:T(8,128)S(1)}, f32[512,17]{0,1:T(8,128)S(1)}, f32[512]{0:T(512)S(1)}, f32[16384]{0:T(1024)S(1)}, /*index=5*/f32[16...) while((s32[]{:T(128)}, f32[512,17]{0,1:T(8,128)S(1)}, ...), condition=%wide.region_123.0_spmd.clone, body=%wide.region_122.0_spmd.clone.sunk | while | flops 325617664 | bytes 6790342 | solution.py:29
  (1306 shorter events, 4285.1 us)
Async XLA Ops:
  7.2 61.2 %all-gather.23.cloned.1.call-start = ((), (), s32[]{:S(2)}) async-start(), calls=%async_computation | async-start | bytes 1622016 | tf_op jit(solution)/shard_map/all_gather | solution.py:41
  7.9 117.0 %all-gather.25.cloned.1.call-start = ((), (), s32[]{:S(2)}) async-start(), calls=%async_computation.1 | async-start | bytes 1622016 | tf_op jit(solution)/shard_map/all_gather | solution.py:46
  9.3 348.7 %all-gather.27.cloned.1.call-start = ((), (), s32[]{:S(2)}) async-start(), calls=%async_computation.2 | async-start | bytes 1622016 | tf_op jit(solution)/shard_map/all_gather | solution.py:46
  262.7 233.2 %copy-start.25 = (f32[17]{0:T(128)}, f32[17]{0:T(128)S(1)}, u32[]{:S(2)}) copy-start(f32[17]{0:T(128)S(1)} %div.126) | copy-start | bytes 208
  303.5 287.7 %all-gather.29.cloned.1.call-start = ((), (), s32[]{:S(2)}) async-start(), calls=%async_computation.3 | async-start | bytes 1622016 | tf_op jit(solution)/shard_map/all_gather | solution.py:46
  536.7 287.7 %all-gather.31.cloned.1.call-start = ((), (), s32[]{:S(2)}) async-start(), calls=%async_computation.4 | async-start | bytes 1622016 | tf_op jit(solution)/shard_map/all_gather | solution.py:46
  769.8 287.7 %all-gather.33.cloned.1.call-start = ((), (), s32[]{:S(2)}) async-start(), calls=%async_computation.5 | async-start | bytes 1622016 | tf_op jit(solution)/shard_map/all_gather | solution.py:46
  1003.0 287.7 %all-gather.35.cloned.1.call-start = ((), (), s32[]{:S(2)}) async-start(), calls=%async_computation.6 | async-start | bytes 1622016 | tf_op jit(solution)/shard_map/all_gather | solution.py:46
  1236.2 287.7 %all-gather.37.cloned.1.call-start = ((), (), s32[]{:S(2)}) async-start(), calls=%async_computation.7 | async-start | bytes 1622016 | tf_op jit(solution)/shard_map/all_gather | solution.py:46
  1469.3 287.7 %all-gather.39.cloned.1.call-start = ((), (), s32[]{:S(2)}) async-start(), calls=%async_computation.8 | async-start | bytes 1622016 | tf_op jit(solution)/shard_map/all_gather | solution.py:46
  1702.4 287.7 %all-gather.41.cloned.1.call-start = ((), (), s32[]{:S(2)}) async-start(), calls=%async_computation.9 | async-start | bytes 1622016 | tf_op jit(solution)/shard_map/all_gather | solution.py:46
  1935.6 287.7 %all-gather.43.cloned.1.call-start = ((), (), s32[]{:S(2)}) async-start(), calls=%async_computation.10 | async-start | bytes 1622016 | tf_op jit(solution)/shard_map/all_gather | solution.py:46
  2168.8 287.7 %all-gather.45.cloned.1.call-start = ((), (), s32[]{:S(2)}) async-start(), calls=%async_computation.11 | async-start | bytes 1622016 | tf_op jit(solution)/shard_map/all_gather | solution.py:46
  2401.9 287.7 %all-gather.47.cloned.1.call-start = ((), (), s32[]{:S(2)}) async-start(), calls=%async_computation.12 | async-start | bytes 1622016 | tf_op jit(solution)/shard_map/all_gather | solution.py:46
  2635.1 287.7 %all-gather.49.cloned.1.call-start = ((), (), s32[]{:S(2)}) async-start(), calls=%async_computation.13 | async-start | bytes 1622016 | tf_op jit(solution)/shard_map/all_gather | solution.py:46
  2868.2 287.7 %all-gather.51.cloned.1.call-start = ((), (), s32[]{:S(2)}) async-start(), calls=%async_computation.14 | async-start | bytes 1622016 | tf_op jit(solution)/shard_map/all_gather | solution.py:46
  3101.4 287.7 %all-gather.53.cloned.1.call-start = ((), (), s32[]{:S(2)}) async-start(), calls=%async_computation.15 | async-start | bytes 1622016 | tf_op jit(solution)/shard_map/all_gather | solution.py:46
  3334.5 287.7 %all-gather.55.cloned.1.call-start = ((), (), s32[]{:S(2)}) async-start(), calls=%async_computation.16 | async-start | bytes 1622016 | tf_op jit(solution)/shard_map/all_gather | solution.py:46
  3567.7 287.7 %all-gather.57.cloned.1.call-start = ((), (), s32[]{:S(2)}) async-start(), calls=%async_computation.17 | async-start | bytes 1622016 | tf_op jit(solution)/shard_map/all_gather | solution.py:46
  3800.9 287.7 %all-gather.59.cloned.1.call-start = ((), (), s32[]{:S(2)}) async-start(), calls=%async_computation.18 | async-start | bytes 1622016 | tf_op jit(solution)/shard_map/all_gather | solution.py:46
  4034.0 287.8 %all-gather.61.cloned.1.call-start = ((), (), s32[]{:S(2)}) async-start(), calls=%async_computation.19 | async-start | bytes 1622016 | tf_op jit(solution)/shard_map/all_gather | solution.py:46
  4088.6 98.5 %copy-start.19 = (f32[512,17]{0,1:T(8,128)S(1)}, f32[512,17]{0,1:T(8,128)}, u32[]{:S(2)}) copy-start(f32[512,17]{0,1:T(8,128)} %multiply_add_fusion.5) | copy-start | bytes 104452
  4267.2 287.8 %all-gather.63.cloned.1.call-start = ((), (), s32[]{:S(2)}) async-start(), calls=%async_computation.20 | async-start | bytes 1622016 | tf_op jit(solution)/shard_map/all_gather | solution.py:46
  4321.8 98.5 %copy-start.20 = (f32[512,17]{0,1:T(8,128)S(1)}, f32[512,17]{0,1:T(8,128)}, u32[]{:S(2)}) copy-start(f32[512,17]{0,1:T(8,128)} %multiply_add_fusion.3) | copy-start | bytes 104452
  4500.4 248.1 %all-gather.65.cloned.1.call-start = ((), (), s32[]{:S(2)}) async-start(), calls=%async_computation.21 | async-start | bytes 1622016 | tf_op jit(solution)/shard_map/all_gather | solution.py:70
  4555.0 98.6 %copy-start.21 = (f32[512,17]{0,1:T(8,128)S(1)}, f32[512,17]{0,1:T(8,128)}, u32[]{:S(2)}) copy-start(f32[512,17]{0,1:T(8,128)} %multiply_add_fusion.1) | copy-start | bytes 104452
  4555.0 138.3 %copy-start.1 = (f32[512,16]{0,1:T(8,128)S(1)}, f32[512,16]{0,1:T(8,128)}, u32[]{:S(2)}) copy-start(f32[512,16]{0,1:T(8,128)} %param.50) | copy-start | bytes 98308
  4555.0 138.3 %copy-start.3 = (f32[512,17]{0,1:T(8,128)S(1)}, f32[512,17]{0,1:T(8,128)}, u32[]{:S(2)}) copy-start(f32[512,17]{0,1:T(8,128)} %multiply_add_fusion.37) | copy-start | bytes 104452
  4555.0 138.3 %copy-start.23 = (f32[512]{0:T(512)S(1)}, f32[512]{0:T(512)}, u32[]{:S(2)}) copy-start(f32[512]{0:T(512)} %param.49) | copy-start | bytes 6148
  4555.0 138.3 %copy-start.26 = (f32[17]{0:T(128)S(1)}, f32[17]{0:T(128)}, u32[]{:S(2)}) copy-start(f32[17]{0:T(128)} %copy-done.25) | copy-start | bytes 208
  4555.0 138.3 %copy-start.28 = (f32[17]{0:T(128)S(1)}, f32[17]{0:T(128)}, u32[]{:S(2)}) copy-start(f32[17]{0:T(128)} %copy-done.27) | copy-start | bytes 208
  4693.5 179.9 %copy-start.24 = (f32[512,1]{0,1:T(1,128)}, f32[512,1]{0,1:T(1,128)S(1)}, u32[]{:S(2)}) copy-start(f32[512,1]{0,1:T(1,128)S(1)} %slice.8) | copy-start | bytes 6148
  (19 other events, 1867.5 us)
Sparse Core Ops, SparseCore 0:
  10.9 57.4 all-gather.22
  71.3 53.5 all-gather.24
  303.6 54.3 all-gather.26
  536.8 54.3 all-gather.28
  770.0 54.3 all-gather.30
  1003.1 54.3 all-gather.32
  1236.3 54.3 all-gather.34
  1469.4 54.3 all-gather.36
  1702.6 54.3 all-gather.38
  1935.7 54.3 all-gather.40
  2168.9 54.3 all-gather.42
  2402.0 54.3 all-gather.44
  2635.2 54.3 all-gather.46
  2868.4 54.3 all-gather.48
  3101.5 54.3 all-gather.50
  3334.7 54.3 all-gather.52
  3567.8 54.3 all-gather.54
  3801.0 54.3 all-gather.56
  4034.1 54.3 all-gather.58
  4267.4 54.3 all-gather.60
  4500.6 54.3 all-gather.62
  4694.3 54.2 all-gather.64
where the time goes:
time: 4950 us; the launch traced here: 4920 us
  matrix products  2070 us (42%)
  blocking collectives  1580 us (32%)
  waiting for transfers between devices  1200 us (24%)
    dot_general x336, matrix products, body(): jnp.dot(kernel, col_right, precision=lax.Precision.HIGHEST, preferred_ele...  1120 us
    all_gather x20, waiting for transfers between devices, apply_kernel(): search_all = lax.all_gather(search_own, 'dp', tiled=True)  1090 us
    dot_general x336, matrix products, body(): lax.dot_general(row_points, col_points, (((1,), (1,)), ((), ())), precisi...  920 us
    psum x19, blocking collectives, local(): new_norm = lax.psum(jnp.sum(residual * residual, axis=0), 'dp')  757 us
    psum x19, blocking collectives, local(): alpha = res_norm / lax.psum(jnp.sum(search * product, axis=0), 'dp')  746 us
  transfers between devices with their start and end apart: 22, of which 22 were waited for; matrix products, arithmetic and copies ran while one was open for 0% of the time, Pallas kernels for 0%

commit v1 on v0

v1 whole, which is shorter than its diff:
```python
import functools
import math

import jax
import jax.numpy as jnp
from jax import lax
from jax.experimental import pallas as pl
from jax.experimental.pallas import tpu as pltpu
from jax.sharding import PartitionSpec as P

CG_STEPS = 20
NDEV = 32
ROWS = 512
GR = 24
NP = 16
KW = 256
KT = 1024
CH = 128
LOG2E = math.log2(math.e)
LN2 = math.log(2.0)
f32 = jnp.float32
bf16 = jnp.bfloat16
MESH = pl.DeviceIdType.MESH


def dot(a, b):
    return lax.dot_general(a, b, (((1,), (0,)), ((), ())), preferred_element_type=f32)


def parts(x):
    h = x.astype(bf16).astype(f32)
    r = x - h
    m = r.astype(bf16).astype(f32)
    return h, m, r - m


def kernel(pay_ref, scal_ref, sol_ref, hyp_ref,
           g0, gq, pall, rall, uall, xk, xi, pp, acc, qown, tsum, tall,
           ha, ma, la, hb, mb, lb, s_send, s_recv, i_send, i_recv, t_send, t_recv):
    me = lax.axis_index("dp")
    n_total = NDEV * ROWS
    out_var = scal_ref[0:1, 0:1]
    noise_var = scal_ref[1:2, 0:1]
    lane_scale = scal_ref[2:3, 0:1]
    row_id = lax.broadcasted_iota(jnp.int32, (GR, 1), 0)
    live = row_id < NP + 1

    def exchange(src, dst_of, send, recv):
        def start(d, c):
            to = lax.rem(me + d, NDEV)
            pltpu.make_async_remote_copy(src_ref=src, dst_ref=dst_of(me), send_sem=send.at[d],
                                         recv_sem=recv.at[me], device_id=(to,), device_id_type=MESH).start()
            return c
        lax.fori_loop(1, NDEV, start, 0)

        def finish(d, c):
            frm = lax.rem(me + NDEV - d, NDEV)
            cp = pltpu.make_async_remote_copy(src_ref=src, dst_ref=dst_of(frm), send_sem=send.at[d],
                                              recv_sem=recv.at[frm], device_id=(frm,), device_id_type=MESH)
            cp.wait_send()
            cp.wait_recv()
            return c
        lax.fori_loop(1, NDEV, finish, 0)

    g0[me] = pay_ref[...]
    exchange(pay_ref, lambda b: g0.at[b], i_send, i_recv)

    aug = pay_ref[0:GR, :]
    own_rows = lax.broadcasted_iota(jnp.int32, (GR, ROWS), 0)
    norm_row = pay_ref[17:18, :]
    side = jnp.where(own_rows < 17, aug * lane_scale, jnp.where(own_rows == 17, 1.0, jnp.where(own_rows == 18, norm_row, 0.0)))
    ih, im, il = parts(side)
    zpad = jnp.zeros((KW - 6 * GR, ROWS), f32)
    xi[...] = jnp.concatenate([ih, im, il, ih, im, ih, zpad], axis=0).astype(bf16)

    def prepare(b, rho):
        kh, km, kl = parts(g0[b, 0:GR, :])
        stacked = jnp.concatenate([kh, kh, kh, km, km, kl, zpad], axis=0)
        xk[pl.ds(pl.multiple_of(b * ROWS, ROWS), ROWS), :] = stacked.T.astype(bf16)
        right = g0[b, GR:2 * GR, :]
        pall[b] = right
        rall[b] = right
        uall[b] = jnp.zeros_like(right)
        put_parts(b, right)
        return rho + right * right

    def put_parts(b, x):
        h, m, l = parts(x)
        both = jnp.concatenate([m, h, l, jnp.zeros((8, ROWS), f32)], axis=0)
        pp[:, pl.ds(pl.multiple_of(b * ROWS, ROWS), ROWS)] = both.astype(bf16)

    zacc = jnp.zeros((GR, ROWS), f32)
    rho0 = jnp.sum(lax.fori_loop(0, NDEV, prepare, zacc), axis=1, keepdims=True)

    bufs = ((ha, ma, la), (hb, mb, lb))

    def product(with_dist):
        def gen(k0, b, c):
            hn, mn, ln = bufs[b]
            s = jnp.minimum(dot(xk[pl.ds(k0 + c, CH), :], xi[...]), 0.0)
            return s

        def put(s, b, c):
            hn, mn, ln = bufs[b]
            o = slice(c, c + CH)
            e = jnp.exp2(s)
            if with_dist:
                e = e * (-LN2 * s)
            hn[o, :] = e.astype(bf16)
            r = e - hn[o, :].astype(f32)
            mn[o, :] = r.astype(bf16)
            ln[o, :] = (r - mn[o, :].astype(f32)).astype(bf16)

        def half(k_new, b_new, k_old, b_old):
            h_, m_, l_ = bufs[b_old]
            a80 = a48 = a32 = None
            for c in range(0, KT, CH):
                o = slice(c, c + CH)
                s = gen(k_new, b_new, c)
                p = pp[:, pl.ds(k_old + c, CH)]
                x, y, z = dot(p, h_[o, :]), dot(p[0:48], m_[o, :]), dot(p[16:48], l_[o, :])
                a80, a48, a32 = (x, y, z) if a80 is None else (a80 + x, a48 + y, a32 + z)
                put(s, b_new, c)
            acc[...] += a80
            acc[0:48, :] += a48
            acc[16:48, :] += a32

        acc[...] = jnp.zeros_like(acc)
        for c in range(0, KT, CH):
            put(gen(0, 0, c), 0, c)

        def body(u, c):
            k = lambda n: pl.multiple_of(lax.rem(2 * u + n, n_total // KT) * KT, KT)
            half(k(1), 1, k(0), 0)
            half(k(2), 0, k(1), 1)
            return c
        lax.fori_loop(0, n_total // KT // 2, body, 0)
        return acc[0:24, :] + acc[24:48, :] + acc[48:72, :]

    def step(i, rho):
        slot = lax.rem(i, 2)
        qown[slot] = out_var * product(False) + noise_var * pall[me]
        gq[slot, me] = qown[slot]
        exchange(qown.at[slot], lambda b: gq.at[slot, b], s_send.at[slot], s_recv.at[slot])
        pq = lax.fori_loop(0, NDEV, lambda b, a: a + pall[b] * gq[slot, b], zacc)
        pq = jnp.sum(pq, axis=1, keepdims=True)
        alpha = jnp.where(live, rho / jnp.where(live, pq, 1.0), 0.0)

        def residual(b, a):
            r = rall[b] - alpha * gq[slot, b]
            rall[b] = r
            uall[b] = uall[b] + alpha * pall[b]
            return a + r * r
        new = jnp.sum(lax.fori_loop(0, NDEV, residual, zacc), axis=1, keepdims=True)
        beta = jnp.where(live, new / jnp.where(live, rho, 1.0), 0.0)

        def search(b, c):
            p = rall[b] + beta * pall[b]
            pall[b] = p
            put_parts(b, p)
            return c
        lax.fori_loop(0, NDEV, search, 0)
        return new
    lax.fori_loop(0, CG_STEPS, step, rho0)

    own_u = uall[me]
    sol_ref[...] = own_u
    is_y = row_id == NP

    def columns(b):
        return jnp.where(is_y, uall[b], g0[b, GR:2 * GR, :])

    def final_parts(b, c):
        put_parts(b, columns(b))
        return c
    lax.fori_loop(0, NDEV, final_parts, 0)
    left = jnp.where(is_y, own_u, own_u * (-1.0 / NP))
    right_own = columns(me)
    own_y = pay_ref[GR:2 * GR, :]
    dist_right = product(True)
    kern_right = product(False)

    def total(x):
        return jnp.sum(jnp.sum(x, axis=1, keepdims=True), axis=0, keepdims=True)
    g_l = out_var * total(left * dist_right)
    g_s = out_var * total(left * kern_right)
    g_n = noise_var * total(left * right_own)
    fit = 0.5 * total(jnp.where(is_y, own_y * own_u, 0.0))
    r8 = lax.broadcasted_iota(jnp.int32, (8, 128), 0)
    tile = jnp.where(r8 == 0, g_l, jnp.where(r8 == 1, g_s, jnp.where(r8 == 2, g_n, jnp.where(r8 == 3, fit, 0.0)))) / n_total
    tsum[...] = tile
    tall[me] = tile
    exchange(tsum, lambda b: tall.at[b], t_send, t_recv)
    hyp_ref[...] = lax.fori_loop(0, NDEV, lambda b, a: a + tall[b], jnp.zeros((8, 128), f32))


def solution(mesh):
    def local(points_own, targets_own, probes_own, log_l, log_s, log_sigma):
        inv_two_l2 = 0.5 * jnp.exp(-2.0 * log_l)
        rate = LOG2E * inv_two_l2
        scal = jnp.stack([jnp.exp(2.0 * log_s), jnp.exp(2.0 * log_sigma), 2.0 * rate])
        scal = jnp.broadcast_to(jnp.pad(scal, (0, 5))[:, None], (8, 128))
        norm = -rate * jnp.sum(points_own * points_own, axis=1)
        one = jnp.ones((1, ROWS), f32)
        pay = jnp.concatenate([points_own.T, norm[None, :], one, jnp.zeros((5, ROWS), f32),
                               probes_own.T, targets_own[None, :], jnp.zeros((7, ROWS), f32)], axis=0)
        dma = pltpu.SemaphoreType.DMA
        sol, hyp = pl.pallas_call(
            kernel,
            out_shape=(jax.ShapeDtypeStruct((GR, ROWS), f32), jax.ShapeDtypeStruct((8, 128), f32)),
            in_specs=[pl.BlockSpec(memory_space=pltpu.VMEM)] * 2,
            out_specs=(pl.BlockSpec(memory_space=pltpu.VMEM),) * 2,
            scratch_shapes=[
                pltpu.VMEM((NDEV, 2 * GR, ROWS), f32),
                pltpu.VMEM((2, NDEV, GR, ROWS), f32),
                pltpu.VMEM((NDEV, GR, ROWS), f32),
                pltpu.VMEM((NDEV, GR, ROWS), f32),
                pltpu.VMEM((NDEV, GR, ROWS), f32),
                pltpu.VMEM((NDEV * ROWS, KW), bf16),
                pltpu.VMEM((KW, ROWS), bf16),
                pltpu.VMEM((80, NDEV * ROWS), bf16),
                pltpu.VMEM((80, ROWS), f32),
                pltpu.VMEM((2, GR, ROWS), f32),
                pltpu.VMEM((8, 128), f32),
                pltpu.VMEM((NDEV, 8, 128), f32),
            ] + [pltpu.VMEM((KT, ROWS), bf16)] * 6 + [
                dma((2, NDEV)), dma((2, NDEV)), dma((NDEV,)), dma((NDEV,)), dma((NDEV,)), dma((NDEV,)),
            ],
            compiler_params=pltpu.CompilerParams(has_side_effects=True, vmem_limit_bytes=60 * 2**20),
            name="gp_cg",
        )(pay, scal)
        return sol[NP], sol[:NP].T, hyp[:4, 0]

    return jax.shard_map(
        local,
        mesh=mesh,
        in_specs=(P("dp", None), P("dp"), P("dp", None), P(), P(), P()),
        out_specs=(P("dp"), P("dp", None), P()),
        check_vma=False,
    )
```

time: 4950 us -> 1270 us (0.26)
  matrix products: 2070 us -> 0 us
  blocking collectives: 1580 us -> 0 us
  Pallas kernels: 0 us -> 1250 us
  waiting for transfers between devices: 1200 us -> 0 us
    dot_general x688 -> x0, matrix products: 2070 us -> none  [the longest x336 1120 us: body(): jnp.dot(kernel, col_right, precision=lax.Precision.HIGHEST, preferred_ele...]
    psum x40 -> x0, blocking collectives: 1580 us -> none  [the longest x19 757 us: local(): new_norm = lax.psum(jnp.sum(residual * residual, axis=0), 'dp')]
    pallas_call x0 -> x1, Pallas kernels: none -> 1250 us  [local(): pl.pallas_call(kernel, out_shape=(jax.ShapeDtypeStruct((GR, ROWS), f32),...]
    all_gather x22 -> x0, waiting for transfers between devices: 1200 us -> none  [the longest x20 1090 us: apply_kernel(): search_all = lax.all_gather(search_own, 'dp', tiled=True)]
  transfers between devices with their start and end apart: 22 -> 0, of which waited for: 22 -> 0; matrix products, arithmetic and copies ran while one was open for 0% -> 0% of each run, Pallas kernels for 0% -> 0%
where the time goes in v1:
time: 1270 us
  Pallas kernels  1250 us (98%)
    pallas_call x1, Pallas kernels, local(): pl.pallas_call(kernel, out_shape=(jax.ShapeDtypeStruct((GR, ROWS), f32),...  1250 us

profile of v1, /device:TPU:0, one launch (start us, length us, event | category | flops | bytes accessed | tf_op | source)
XLA Modules:
  0.0 1266.5 jit_solution(10904840331066194460)
XLA Ops:
  2.7 0.1 select_maximum_fusion
  2.8 0.0 copy-start
  2.8 0.9 multiply_reduce_fusion
  3.7 0.0 copy-start.1
  3.7 0.7 broadcast_in_dim.23.scal_ref
  4.4 0.0 copy-start.2
  4.4 0.0 copy-done
  4.4 0.1 copy-done.1
  4.4 0.6 copy-done.2
  5.0 3.2 concatenate.3.pay_ref
  8.2 1254.3 %gp_cg.1 = (f32[24,512]{1,0:T(8,128)}, f32[8,128]{1,0:T(8,128)}) custom-call(f32[48,512]{1,0:T(8,128)} %concatenate.3.pay_ref, f32[8,128]{1,0:T(8,128)} %broadcast_in_dim.23.scal_ref), custom_call_target="tpu_custom_call" | custom-call | tf_op jit(solution)/shard_map/gp_cg/pallas_call | solution.py:208
  1262.5 1.3 slice_reduce_fusion
  1263.8 1.3 slice.9
  1265.1 1.4 slice_bitcast_fusion
  (4 shorter events, 0.0 us)
Async XLA Ops:
  2.8 1.6 copy-start
  3.7 0.8 copy-start.1
  4.4 0.7 copy-start.2

commit v2 on v0

v2 whole, which is shorter than its diff:
```python
import math

import jax
import jax.numpy as jnp
import numpy as np
from jax import lax
from jax.experimental import pallas as pl
from jax.experimental.pallas import tpu as pltpu
from jax.sharding import PartitionSpec as P

CG_STEPS = 20
NDEV = 32
ROWS = 512
HALF = 256
NP = 16
DIM = 17
N = NDEV * ROWS
PRE = 12288
REST = N - PRE
LOG2E = math.log2(math.e)
LN2 = math.log(2.0)
f32 = jnp.float32
bf16 = jnp.bfloat16
MESH = pl.DeviceIdType.MESH

TERMS = ((0, 0), (0, 1), (0, 2), (1, 0), (1, 1), (2, 0))


def placements():
    col, row, right, left = (np.zeros((72, 128), np.float32) for _ in range(4))
    j = 0
    for a, b in TERMS:
        for d in range(DIM):
            col[24 * a + d, j] = row[24 * b + d, j] = 1.0
            j += 1
    for t in range(3):
        col[24 * t + 17, j] = row[18, j] = 1.0
        j += 1
    for t in range(3):
        col[18, j] = row[24 * t + 17, j] = 1.0
        j += 1
    j = 0
    for t in range(3):
        for d in range(NP):
            right[d, j] = left[24 * t + d, j] = 1.0
            j += 1
    for a, b in TERMS:
        right[24 * a + NP, j] = left[24 * b + NP, j] = 1.0
        j += 1
    return np.stack([col, row, right, left])


def dot(a, b):
    return lax.dot_general(a, b, (((1,), (0,)), ((), ())), preferred_element_type=f32)


def dot_t(a, b):
    return lax.dot_general(a, b, (((0,), (0,)), ((), ())), preferred_element_type=f32)


def parts(x):
    h = x.astype(bf16).astype(f32)
    r = x - h
    m = r.astype(bf16).astype(f32)
    return h, m, r - m


def wide(v):
    first = lax.broadcasted_iota(jnp.int32, (8, 128), 0) == 0
    y0 = jnp.where(first, v[4], 0.0)
    y1 = jnp.where(first, pltpu.roll(v[4], 7, 0), 0.0)
    top = jnp.concatenate([v[0], v[2], y0], axis=0)
    return jnp.concatenate([top, jnp.concatenate([v[1], v[3], y1], axis=0)], axis=1)


def narrow(q):
    row = lax.broadcasted_iota(jnp.int32, (8, 128), 0)
    y0, y1 = q[16:24, 0:128], q[16:24, 128:256]
    y = jnp.where(row == 0, y0, jnp.where(row == 1, pltpu.roll(y1, 1, 0), 0.0))
    return jnp.stack([q[0:8, 0:128], q[0:8, 128:256], q[8:16, 0:128], q[8:16, 128:256], y])


def kernel(pay_ref, scal_ref, place_ref, sol_ref, hyp_ref,
           gq, zall, pall, rall, uall, xk, xi, pp, acc, qown, tsum, tall,
           ph, pm, pl_, rh, rm, rl, send, recv, t_send, t_recv):
    me = lax.axis_index("dp")
    sib = me + 1 - 2 * lax.rem(me, 2)
    out_var = scal_ref[0:1, 0:1]
    noise_var = scal_ref[1:2, 0:1]
    rate = scal_ref[2:3, 0:1]

    def flip(i, bit):
        return i + bit - 2 * bit * lax.rem(i // bit, 2)

    def shift_z(i, k):
        return lax.rem(i // 8 + k, 4) * 8 + lax.rem(i, 8)

    nbrs = (flip(me, 2), flip(me, 4), flip(flip(me, 2), 4))

    class Gather:
        def __init__(self, slot, h, src, into=None):
            self.slot, self.h, self.src, self.k = slot, h, src, 0
            self.into = into or (lambda block: gq.at[slot, h, block])

        def copy(self, block, src, to, k):
            return pltpu.make_async_remote_copy(
                src_ref=src, dst_ref=self.into(block), send_sem=send.at[self.h, k],
                recv_sem=recv.at[self.slot, self.h, block], device_id=(to,), device_id_type=MESH)

        def put(self, block, src, to):
            self.copy(block, src, to, self.k).start()
            self.k += 1

        def arrived(self, block):
            self.copy(block, self.src, sib, 0).wait_recv()
            return self.into(block)

        def own(self):
            for dz in (1, 3, 2):
                self.put(me, self.src, shift_z(me, dz))
            for t in nbrs:
                self.put(me, self.src, t)
            self.put(me, self.src, sib)

        def lines(self):
            for dz in (1, 3, 2):
                b = shift_z(me, dz)
                src = self.arrived(b)
                for t in nbrs:
                    self.put(b, src, t)
                self.put(b, src, sib)

        def planes(self):
            for dz in (0, 1, 3, 2):
                for t in nbrs:
                    b = shift_z(t, dz)
                    self.put(b, self.arrived(b), sib)

        def finish(self):
            def wait_in(d, c):
                self.arrived(lax.rem(sib + 2 * d, NDEV))
                return c
            lax.fori_loop(0, NDEV // 2, wait_in, 0)

            def wait_out(k, c):
                self.copy(me, self.src, sib, k).wait_send()
                return c
            lax.fori_loop(0, self.k, wait_out, 0)

    def split_to(e, hr, mr, lr, idx):
        hr[idx] = e.astype(bf16)
        r = e - hr[idx].astype(f32)
        mr[idx] = r.astype(bf16)
        lr[idx] = (r - mr[idx].astype(f32)).astype(bf16)

    def ahead(k0, rows, chunk=256, sub=64):
        for c in range(0, rows, chunk):
            s = dot(xk[pl.ds(k0 + c, chunk), :], xi[...])
            for r in range(0, chunk, sub):
                for h in (0, 1):
                    e = jnp.exp2(jnp.minimum(s[r:r + sub, h * HALF:(h + 1) * HALF], 0.0))
                    split_to(e, ph, pm, pl_, (h, pl.ds(k0 + c + r, sub), slice(None)))

    def apply(h, k0, rows, bufs):
        p = jnp.concatenate([pp[:, pl.ds(k0, rows)], jnp.zeros((48, rows), bf16)], axis=0)
        a = dot(p, bufs[0]) + dot(p, bufs[1]) + dot(p, bufs[2])
        return a[0:72]

    TILE, NEW = 3072, 1024

    def half_product(h):
        acc[...] = jnp.zeros_like(acc)
        lanes = pl.ds(h * HALF, HALF)

        def body(i, c):
            k0 = pl.multiple_of(i * TILE, TILE)
            n0 = pl.multiple_of(i * NEW, NEW)
            total = None
            for j in range(4):
                s = dot(xk[pl.ds(PRE + n0 + j * 256, 256), :], xi[:, lanes])
                kk, w = k0 + j * (TILE // 4), TILE // 4
                a = apply(h, kk, w, [ref[h, pl.ds(kk, w), :] for ref in (ph, pm, pl_)])
                total = a if total is None else total + a
                for r in range(0, 256, 64):
                    e = jnp.exp2(jnp.minimum(s[r:r + 64, :], 0.0))
                    split_to(e, rh, rm, rl, (pl.ds(n0 + j * 256 + r, 64), slice(None)))
            acc[...] += total
            return c
        lax.fori_loop(0, PRE // TILE, body, 0)
        a = apply(h, PRE, REST, [ref[...] for ref in (rh, rm, rl)]) + acc[...]
        return a[0:24] + a[24:48] + a[48:72]

    for h in (0, 1):
        uall[me, h] = pay_ref[0, h]
        gq[1, h, me] = pay_ref[1, h]
    xs = [Gather(0, h, pay_ref.at[0, h], lambda b, h=h: uall.at[b, h]) for h in (0, 1)]
    for g in xs:
        g.own()
    for g in xs:
        g.lines()
    for g in xs:
        g.planes()
    for g in xs:
        g.finish()
    row24 = lax.broadcasted_iota(jnp.int32, (24, HALF), 0)

    def augmented(v, scale):
        w = wide(v)
        norm = -rate * jnp.sum(w * w, axis=0, keepdims=True)
        return jnp.where(row24 == 17, norm, jnp.where(row24 == 18, 1.0, w * scale))

    def stack(x):
        return jnp.concatenate(parts(x), axis=0).astype(bf16)

    for h in (0, 1):
        side = stack(augmented(pay_ref[0, h], 2.0 * rate))
        xi[:, h * HALF:(h + 1) * HALF] = dot_t(place_ref[1], side).astype(bf16)

    def pack_points(b, c):
        for h in (0, 1):
            x = stack(augmented(uall[b, h], 1.0))
            xk[pl.ds(pl.multiple_of(b * ROWS + h * HALF, HALF), HALF), :] = dot_t(x, place_ref[0]).astype(bf16)
        return c

    bs = [Gather(1, h, pay_ref.at[1, h]) for h in (0, 1)]
    for g in bs:
        g.own()
    lax.fori_loop(0, NDEV, pack_points, 0)
    AHEAD = 2048

    def ahead_loop(lo, hi):
        def body(i, c):
            ahead(pl.multiple_of(i * AHEAD, AHEAD), AHEAD)
            return c
        lax.fori_loop(lo, hi, body, 0)

    for g in bs:
        g.lines()
    ahead_loop(0, 3)
    for g in bs:
        g.planes()
    ahead_loop(3, 6)
    for g in bs:
        g.finish()

    def put_parts(b, h, v):
        a, m, l = parts(wide(v))
        both = jnp.concatenate([m, a, l, jnp.zeros((8, HALF), f32)], axis=0)
        pp[:, pl.ds(pl.multiple_of(b * ROWS + h * HALF, HALF), HALF)] = both.astype(bf16)

    zero5 = jnp.zeros((5, 8, 128), f32)

    def column_sums(x):
        both = jnp.concatenate([x[0] + x[1], x[2] + x[3], x[4]], axis=0)
        s = jnp.sum(both, axis=1, keepdims=True)
        return s[0:8], s[8:16], s[16:17] + s[17:18]

    def spread(s):
        a, b, y = (jnp.broadcast_to(x, (8, 128)) for x in s)
        return jnp.stack([a, a, b, b, y])

    def begin(b, a):
        for h in (0, 1):
            v = gq[1, h, b]
            zall[b, h] = v
            pall[b, h] = v
            rall[b, h] = v
            uall[b, h] = jnp.zeros_like(v)
            put_parts(b, h, v)
            a = a + v * v
        return a
    rho0 = column_sums(lax.fori_loop(0, NDEV, begin, zero5))

    def step(i, rho):
        slot = lax.rem(i, 2)
        gs = []
        for h in (0, 1):
            q = narrow(half_product(h))
            qown[slot, h] = out_var * q + noise_var * pall[me, h]
            gq[slot, h, me] = qown[slot, h]
            g = Gather(slot, h, qown.at[slot, h])
            g.own()
            gs.append(g)
        gs[0].lines()
        ahead_loop(0, 3)
        gs[0].planes()
        gs[1].lines()
        ahead_loop(3, 6)
        gs[1].planes()
        gs[0].finish()
        gs[1].finish()

        def inner(b, a):
            for h in (0, 1):
                a = a + pall[b, h] * gq[slot, h, b]
            return a
        pq = column_sums(lax.fori_loop(0, NDEV, inner, zero5))
        alpha = spread([r / q for r, q in zip(rho, pq)])

        def residual(b, a):
            for h in (0, 1):
                r = rall[b, h] - alpha * gq[slot, h, b]
                rall[b, h] = r
                uall[b, h] = uall[b, h] + alpha * pall[b, h]
                a = a + r * r
            return a
        new = column_sums(lax.fori_loop(0, NDEV, residual, zero5))
        beta = spread([n / r for n, r in zip(new, rho)])

        def search(b, c):
            for h in (0, 1):
                p = rall[b, h] + beta * pall[b, h]
                pall[b, h] = p
                put_parts(b, h, p)
            return c
        lax.fori_loop(0, NDEV, search, 0)
        return new
    lax.fori_loop(0, CG_STEPS, step, rho0)

    ids = lax.broadcasted_iota(jnp.int32, (5, 8, 128), 0)
    is_y = ids == 4
    own_sum = jnp.zeros((5, 8, 128), f32)
    fit_sum = jnp.zeros((5, 8, 128), f32)
    for h in (0, 1):
        u = uall[me, h]
        z = zall[me, h]
        sol_ref[h] = u
        left = jnp.where(is_y, u, u * (-1.0 / NP))
        own_sum = own_sum + left * jnp.where(is_y, u, z)
        fit_sum = fit_sum + jnp.where(is_y, u * z, 0.0)
        pp[:, h * HALF:(h + 1) * HALF] = jnp.zeros((80, HALF), bf16)
        ai = dot_t(place_ref[3], stack(wide(left))).astype(bf16)
        pp[0:64, h * HALF:(h + 1) * HALF] = ai[0:64]

    def pair_sums(b, carry):
        a_s, a_l = carry
        for h in (0, 1):
            right = jnp.where(is_y, uall[b, h], zall[b, h])
            ck = dot_t(stack(wide(right)), place_ref[2]).astype(bf16)
            k0 = pl.multiple_of(b * ROWS + h * HALF, HALF)
            s = dot(xk[pl.ds(k0, HALF), :], xi[...])
            g = dot(ck[:, 0:64], pp[0:64, 0:ROWS])
            for r in range(0, HALF, 8):
                sr = jnp.minimum(s[r:r + 8], 0.0)
                t = jnp.exp2(sr) * g[r:r + 8]
                a_s = a_s + t
                a_l = a_l + t * sr
        return a_s, a_l
    zrow = jnp.zeros((8, ROWS), f32)
    a_s, a_l = lax.fori_loop(0, NDEV, pair_sums, (zrow, zrow))

    def total(x):
        return jnp.sum(jnp.sum(x, axis=1, keepdims=True), axis=0, keepdims=True)

    def total5(x):
        return total(x[0] + x[1] + x[2] + x[3] + x[4])
    g_l = out_var * (-LN2) * total(a_l)
    g_s = out_var * total(a_s)
    g_n = noise_var * total5(own_sum)
    fit = 0.5 * total5(fit_sum)
    r8 = lax.broadcasted_iota(jnp.int32, (8, 128), 0)
    tile = jnp.where(r8 == 0, g_l, jnp.where(r8 == 1, g_s, jnp.where(r8 == 2, g_n, jnp.where(r8 == 3, fit, 0.0)))) / N
    tsum[...] = tile
    tall[me] = tile

    def t_copy(to, block, k):
        return pltpu.make_async_remote_copy(src_ref=tsum, dst_ref=tall.at[block], send_sem=t_send.at[k],
                                            recv_sem=t_recv.at[block], device_id=(to,), device_id_type=MESH)

    def t_start(d, c):
        t_copy(lax.rem(me + d, NDEV), me, d).start()
        return c
    lax.fori_loop(1, NDEV, t_start, 0)

    def t_finish(d, c):
        cp = t_copy(sib, lax.rem(me + d, NDEV), d)
        cp.wait_send()
        cp.wait_recv()
        return c
    lax.fori_loop(1, NDEV, t_finish, 0)
    hyp_ref[...] = lax.fori_loop(0, NDEV, lambda b, a: a + tall[b], jnp.zeros((8, 128), f32))


def to_half_blocks(main, last):
    m = main.reshape(2, 8, 2, 2, 128).transpose(2, 0, 3, 1, 4).reshape(2, 4, 8, 128)
    y = jnp.pad(last.reshape(2, 1, 2, 128), ((0, 0), (0, 0), (0, 6), (0, 0)))
    return jnp.concatenate([m, y], axis=1)


def solution(mesh):
    def local(points_own, targets_own, probes_own, log_l, log_s, log_sigma):
        rate = LOG2E * 0.5 * jnp.exp(-2.0 * log_l)
        scal = jnp.stack([jnp.exp(2.0 * log_s), jnp.exp(2.0 * log_sigma), rate])
        scal = jnp.broadcast_to(jnp.pad(scal, (0, 5))[:, None], (8, 128))
        xt = points_own.T
        pay = jnp.stack([to_half_blocks(xt[:16], xt[16]), to_half_blocks(probes_own.T, targets_own)])
        dma = pltpu.SemaphoreType.DMA
        blocks = pltpu.VMEM((NDEV, 2, 5, 8, 128), f32)
        sol, hyp = pl.pallas_call(
            kernel,
            out_shape=(jax.ShapeDtypeStruct((2, 5, 8, 128), f32), jax.ShapeDtypeStruct((8, 128), f32)),
            in_specs=[pl.BlockSpec(memory_space=pltpu.VMEM)] * 3,
            out_specs=(pl.BlockSpec(memory_space=pltpu.VMEM),) * 2,
            scratch_shapes=[
                pltpu.VMEM((2, 2, NDEV, 5, 8, 128), f32),
                blocks, blocks, blocks, blocks,
                pltpu.VMEM((N, 128), bf16),
                pltpu.VMEM((128, ROWS), bf16),
                pltpu.VMEM((80, N), bf16),
                pltpu.VMEM((72, HALF), f32),
                pltpu.VMEM((2, 2, 5, 8, 128), f32),
                pltpu.VMEM((8, 128), f32),
                pltpu.VMEM((NDEV, 8, 128), f32),
            ] + [pltpu.VMEM((2, PRE, HALF), bf16)] * 3 + [pltpu.VMEM((REST, HALF), bf16)] * 3 + [
                dma((2, NDEV)), dma((2, 2, NDEV)), dma((NDEV,)), dma((NDEV,)),
            ],
            compiler_params=pltpu.CompilerParams(has_side_effects=True, vmem_limit_bytes=67043328),
            name="gp_cg",
        )(pay, scal, jnp.asarray(placements(), bf16))
        v = sol[:, :4].reshape(2, 2, 2, 8, 128).transpose(0, 2, 4, 1, 3).reshape(ROWS, NP)
        u = sol[:, 4, :2].reshape(ROWS)
        return u, v, hyp[:4, 0]

    return jax.shard_map(
        local,
        mesh=mesh,
        in_specs=(P("dp", None), P("dp"), P("dp", None), P(), P(), P()),
        out_specs=(P("dp"), P("dp", None), P()),
        check_vma=False,
    )
```

time: 4950 us -> 550 us (0.11)
  matrix products: 2070 us -> 0 us
  blocking collectives: 1580 us -> 0 us
  waiting for transfers between devices: 1200 us -> 0 us
  Pallas kernels: 0 us -> 540 us
    dot_general x688 -> x0, matrix products: 2070 us -> none  [the longest x336 1120 us: body(): jnp.dot(kernel, col_right, precision=lax.Precision.HIGHEST, preferred_ele...]
    psum x40 -> x0, blocking collectives: 1580 us -> none  [the longest x19 757 us: local(): new_norm = lax.psum(jnp.sum(residual * residual, axis=0), 'dp')]
    all_gather x22 -> x0, waiting for transfers between devices: 1200 us -> none  [the longest x20 1090 us: apply_kernel(): search_all = lax.all_gather(search_own, 'dp', tiled=True)]
    pallas_call x0 -> x1, Pallas kernels: none -> 540 us  [local(): pl.pallas_call(kernel, out_shape=(jax.ShapeDtypeStruct((2, 5, 8, 128), f3...]
  transfers between devices with their start and end apart: 22 -> 0, of which waited for: 22 -> 0; matrix products, arithmetic and copies ran while one was open for 0% -> 0% of each run, Pallas kernels for 0% -> 0%
where the time goes in v2:
time: 550 us
  Pallas kernels  540 us (98%)
  local copies, waits for them, and re-layouts  6.16 us (1%)
    pallas_call x1, Pallas kernels, local(): pl.pallas_call(kernel, out_shape=(jax.ShapeDtypeStruct((2, 5, 8, 128), f3...  540 us

profile of v2, /device:TPU:0, one launch (start us, length us, event | category | flops | bytes accessed | tf_op | source)
XLA Modules:
  0.0 549.5 jit_solution(2243829513619634400)
XLA Ops:
  0.6 0.8 slice.20
  1.4 0.0 copy-start
  1.4 0.7 slice.21
  2.1 0.0 copy-done
  2.2 0.0 copy-start.1
  2.2 0.7 copy-done.1
  2.8 0.6 pad_maximum_fusion.pay_ref
  5.5 0.1 select_maximum_fusion.2
  5.6 0.7 broadcast_in_dim.2.scal_ref
  6.3 539.9 %gp_cg.1 = (f32[2,5,8,128]{3,2,1,0:T(8,128)}, f32[8,128]{1,0:T(8,128)}) custom-call(f32[2,2,5,8,128]{4,3,2,1,0:T(8,128)} %pad_maximum_fusion.pay_ref, f32[8,128]{1,0:T(8,128)} %broadcast_in_dim.2.scal_ref, bf16[4,72,128]{2,1,0:T(8,128)(2,1)} %constant.11.clone.place_ref), custom_call_target="tpu_custom_call" | custom-call | tf_op jit(solution)/shard_map/gp_cg/pallas_call | solution.py:399
  546.2 0.8 slice.18
  547.0 0.6 copy.15
  547.6 0.0 copy-start.2
  547.6 1.3 slice.17
  548.9 0.0 copy-done.2
  548.9 0.6 slice_reduce_fusion
  (3 shorter events, 0.0 us)
Async XLA Ops:
  1.4 0.8 copy-start
  2.2 0.7 copy-start.1
  547.6 1.3 copy-start.2

commit v3 on v0

v3 whole, which is shorter than its diff:
```python
import math

import jax
import jax.numpy as jnp
import numpy as np
from jax import lax
from jax.experimental import pallas as pl
from jax.experimental.pallas import tpu as pltpu
from jax.sharding import PartitionSpec as P

CG_STEPS = 20
NDEV = 32
ROWS = 512
HALF = 256
NP = 16
DIM = 17
N = NDEV * ROWS
PLANE = 8 * ROWS
ORDER = (0, 1, 3, 2)
WINDOW = (("ahead", 0, 0, 0, 4096), ("line", 1), ("plane", 0), ("ahead", 2, 2, 0, 2048), ("line", 3), ("line", 2),
          ("ahead", 2, 2, 2048, 4096))
BODY = (("rest", 0), ("update", 0), ("apply", 0), ("plane", 1), ("ahead", 3, 0, 0, 2048), ("rest", 1), ("update", 1),
        ("plane", 3), ("apply", 1), ("plane", 2), ("rest", 3), ("update", 3),
        ("apply", 2, (3, 0, 2048, 4096), (1, 1, 0, 1024)), ("rest", 2), ("sent",), ("update", 2), ("rho",),
        ("apply", 0, (1, 1, 1024, 4096)))
LOG2E = math.log2(math.e)
LN2 = math.log(2.0)
f32 = jnp.float32
bf16 = jnp.bfloat16
MESH = pl.DeviceIdType.MESH

TERMS = ((0, 0), (0, 1), (0, 2), (1, 0), (1, 1), (2, 0))


def placements():
    col, row, right, left = (np.zeros((72, 128), np.float32) for _ in range(4))
    j = 0
    for a, b in TERMS:
        for d in range(DIM):
            col[24 * a + d, j] = row[24 * b + d, j] = 1.0
            j += 1
    for t in range(3):
        col[24 * t + 17, j] = row[18, j] = 1.0
        j += 1
    for t in range(3):
        col[18, j] = row[24 * t + 17, j] = 1.0
        j += 1
    j = 0
    for t in range(3):
        for d in range(NP):
            right[d, j] = left[24 * t + d, j] = 1.0
            j += 1
    for a, b in TERMS:
        right[24 * a + NP, j] = left[24 * b + NP, j] = 1.0
        j += 1
    return np.stack([col, row, right, left])


def dot(a, b):
    return lax.dot_general(a, b, (((1,), (0,)), ((), ())), preferred_element_type=f32)


def dot_t(a, b):
    return lax.dot_general(a, b, (((0,), (0,)), ((), ())), preferred_element_type=f32)


def parts(x):
    h = x.astype(bf16).astype(f32)
    r = x - h
    m = r.astype(bf16).astype(f32)
    return h, m, r - m


def wide(v):
    first = lax.broadcasted_iota(jnp.int32, (8, 128), 0) == 0
    last = [jnp.where(first, v[8] if t == 0 else pltpu.roll(v[8], 8 - t, 0), 0.0) for t in range(4)]
    return jnp.concatenate([jnp.concatenate([v[t], v[4 + t], last[t]], axis=0) for t in range(4)], axis=1)


def narrow(q):
    row = lax.broadcasted_iota(jnp.int32, (8, 128), 0)
    last = jnp.zeros((8, 128), f32)
    for t in range(4):
        y = q[16:24, t * 128:(t + 1) * 128]
        last = jnp.where(row == t, y if t == 0 else pltpu.roll(y, t, 0), last)
    return jnp.stack([q[8 * g:8 * g + 8, t * 128:(t + 1) * 128] for g in (0, 1) for t in range(4)] + [last])


def kernel(pay_ref, scal_ref, place_ref, sol_ref, hyp_ref,
           gq, rall, pyall, uyall, pown, uown, xk, xi, pp, acc, qown, tsum, tall,
           h0, m0, l0, h1, m1, l1, h2, m2, l2, send, recv, t_send, t_recv):
    me = lax.axis_index("dp")
    core = lax.rem(me, 2)
    sib = me + 1 - 2 * core
    out_var = scal_ref[0:1, 0:1]
    noise_var = scal_ref[1:2, 0:1]
    rate = scal_ref[2:3, 0:1]
    slots = ((h0, m0, l0), (h1, m1, l1), (h2, m2, l2))

    def flip(i, bit):
        return i + bit - 2 * bit * lax.rem(i // bit, 2)

    def shift_z(i, k):
        return lax.rem(i // 8 + k, 4) * 8 + lax.rem(i, 8)

    def plane_of(k):
        return lax.rem(me // 8 + k, 4)

    nbrs = (flip(me, 2), flip(me, 4), flip(flip(me, 2), 4))
    sib_plane = (sib, flip(sib, 2), flip(sib, 4), flip(flip(sib, 2), 4))

    class Gather:
        def __init__(self, slot, src, into=None):
            self.slot, self.src = slot, src
            self.into = into or (lambda block: gq.at[slot, block])

        def copy(self, block, src, to):
            return pltpu.make_async_remote_copy(
                src_ref=src, dst_ref=self.into(block), send_sem=send.at[0],
                recv_sem=recv.at[self.slot, block], device_id=(to,), device_id_type=MESH)

        def arrived(self, block):
            self.copy(block, self.src, sib).wait_recv()
            return self.into(block)

        def own(self):
            for dz in (1, 3, 2):
                self.copy(me, self.src, shift_z(me, dz)).start()
            for t in nbrs:
                self.copy(me, self.src, t).start()
            self.copy(me, self.src, sib).start()

        def line(self, dz):
            b = shift_z(me, dz)
            src = self.arrived(b)
            for t in nbrs:
                self.copy(b, src, t).start()
            self.copy(b, src, sib).start()

        def plane(self, dz):
            for t in nbrs:
                b = shift_z(t, dz)
                self.copy(b, self.arrived(b), sib).start()

        def rest(self, dz):
            for t in sib_plane:
                self.arrived(shift_z(t, dz))

        def sent(self):
            many = gq.at[0, pl.ds(0, NDEV - 1)]
            pltpu.make_async_remote_copy(src_ref=many, dst_ref=many, send_sem=send.at[0], recv_sem=recv.at[self.slot, me],
                                         device_id=(sib,), device_id_type=MESH).wait_send()

    def split_to(e, bufs, idx):
        hr, mr, lr = bufs
        hr[idx] = e.astype(bf16)
        r = e - hr[idx].astype(f32)
        mr[idx] = r.astype(bf16)
        lr[idx] = (r - mr[idx].astype(f32)).astype(bf16)

    def entries(s, bufs, c, sub=64):
        for r in range(0, s.shape[0], sub):
            for h in (0, 1):
                e = jnp.exp2(jnp.minimum(s[r:r + sub, h * HALF:(h + 1) * HALF], 0.0))
                split_to(e, bufs, (h, pl.ds(c + r, sub), slice(None)))

    def ahead(dz, slot, lo, hi, rows=2048):
        base = plane_of(dz) * PLANE

        def body(i, c):
            c0 = pl.multiple_of(i * rows, rows)
            for j in range(0, rows, 256):
                entries(dot(xk[pl.ds(base + c0 + j, 256), :], xi[...]), slots[slot], c0 + j)
            return c
        lax.fori_loop(lo // rows, hi // rows, body, 0)

    def apply(slot, new):
        todo = [(plane_of(dz) * PLANE, slots[to], c) for dz, to, lo, hi in new for c in range(lo, hi, 256)]
        for h in (0, 1):
            mine = todo[h * len(todo) // 2:(h + 1) * len(todo) // 2]
            subs = max(1, len(mine))
            cuts = [256 * (PLANE // 256 * j // subs) for j in range(subs + 1)]
            total = None
            for j in range(subs):
                if mine:
                    base, bufs, col = mine[j]
                    s = dot(xk[pl.ds(base + col, 256), :], xi[...])
                kk, w = cuts[j], cuts[j + 1] - cuts[j]
                p = jnp.concatenate([pp[:, kk:kk + w], jnp.zeros((48, w), bf16)], axis=0)
                for ref in slots[slot]:
                    d = dot(p, ref[h, kk:kk + w, :])
                    total = d if total is None else total + d
                if mine:
                    entries(s, bufs, col)
            acc[:, h * HALF:(h + 1) * HALF] += total[0:72]

    row24 = lax.broadcasted_iota(jnp.int32, (24, ROWS), 0)

    def augmented(v, scale):
        w = wide(v)
        norm = -rate * jnp.sum(w * w, axis=0, keepdims=True)
        return jnp.where(row24 == 17, norm, jnp.where(row24 == 18, 1.0, w * scale))

    def stack(x):
        return jnp.concatenate(parts(x), axis=0).astype(bf16)

    zero9 = jnp.zeros((9, 8, 128), f32)
    rall[me] = pay_ref[0]
    gq[2, me] = pay_ref[1]
    xs = Gather(0, pay_ref.at[0], lambda b: rall.at[b])
    bs = Gather(2, pay_ref.at[1])
    xs.own()
    xi[...] = dot_t(place_ref[1], stack(augmented(pay_ref[0], 2.0 * rate))).astype(bf16)
    xs.plane(0)
    for dz in (1, 3, 2):
        xs.line(dz)
    for dz in (1, 3, 2):
        xs.plane(dz)
    for dz in ORDER:
        xs.rest(dz)
    xs.sent()

    def pack_points(b, c):
        x = stack(augmented(rall[b], 1.0))
        xk[pl.ds(pl.multiple_of(b * ROWS, ROWS), ROWS), :] = dot_t(x, place_ref[0]).astype(bf16)
        rall[b] = zero9
        pyall[b] = jnp.zeros((8, 128), f32)
        uyall[b] = jnp.zeros((8, 128), f32)
        return c

    bs.own()
    lax.fori_loop(0, NDEV, pack_points, 0)
    pown[...] = zero9
    uown[...] = zero9
    bs.plane(0)
    for dz in (1, 3, 2):
        bs.line(dz)
    for j in (0, 1, 2):
        ahead(ORDER[j], j, 0, PLANE)

    def column_sums(x):
        both = jnp.concatenate([x[0] + x[1] + (x[2] + x[3]), x[4] + x[5] + (x[6] + x[7]), x[8]], axis=0)
        s = jnp.sum(both, axis=1, keepdims=True)
        y = s[16:17] + s[17:18] + (s[18:19] + s[19:20])
        return jnp.concatenate([s[0:16], jnp.broadcast_to(y, (8, 1))], axis=0)

    def spread(s):
        a, b, y = (jnp.broadcast_to(s[j:j + 8], (8, 128)) for j in (0, 8, 16))
        return jnp.stack([a] * 4 + [b] * 4 + [y])


    lane_of_row = lax.broadcasted_iota(jnp.int32, (24, 128), 1) == lax.broadcasted_iota(jnp.int32, (24, 128), 0)

    def share(slot, values):
        row = jnp.sum(jnp.where(lane_of_row, values, 0.0), axis=0, keepdims=True)
        tsum[slot, 0:1] = row
        tall[slot, me, 0:1] = row
        for d in range(1, NDEV):
            pltpu.make_async_remote_copy(src_ref=tsum.at[slot, 0:1], dst_ref=tall.at[slot, me, 0:1], send_sem=t_send.at[0],
                                         recv_sem=t_recv.at[slot], device_id=(lax.rem(me + d, NDEV),),
                                         device_id_type=MESH).start()

    def shared(slot):
        many = tall.at[slot, pl.ds(0, NDEV - 1), 0:1]
        cp = pltpu.make_async_remote_copy(src_ref=many, dst_ref=many, send_sem=t_send.at[0], recv_sem=t_recv.at[slot],
                                          device_id=(sib,), device_id_type=MESH)
        cp.wait_send()
        cp.wait_recv()
        t = [tall[slot, b, 0:1] for b in range(NDEV)]
        while len(t) > 1:
            t = [t[j] + t[j + 1] for j in range(0, len(t), 2)]
        return jnp.sum(jnp.where(lane_of_row, t[0], 0.0), axis=1, keepdims=True)

    def last_column(b, r, alpha, beta):
        p = r + beta[8] * pyall[b]
        pyall[b] = p
        uyall[b] = uyall[b] + alpha[8] * p

    def step(i, carry):
        alpha, beta, rho = carry
        slot = lax.rem(i, 2)
        before = lax.rem(i + 1, 2) + 1 - (i + NDEV - 1) // NDEV
        g = Gather(before, qown.at[before])
        acc[...] = jnp.zeros_like(acc)

        def update(dz, total):
            for j in range(8):
                b = plane_of(dz) * 8 + j
                old = rall[b]
                last_column(b, old[8], alpha, beta)
                r = old - alpha * gq[before, b]
                rall[b] = r
                a, m, l = parts(wide(r))
                both = jnp.concatenate([m, a, l, jnp.zeros((8, ROWS), f32)], axis=0)
                pp[:, j * ROWS:(j + 1) * ROWS] = both.astype(bf16)
                total = total + r * r
            return total

        total = zero9
        for op, *arg in BODY:
            if op == "update":
                total = update(arg[0], total)
            elif op == "rho":
                new = spread(column_sums(total))
                beta = new / rho
            elif op == "apply":
                apply(arg[0], [(ORDER[n[0]],) + n[1:] for n in arg[1:]])
            elif op == "ahead":
                ahead(ORDER[arg[0]], *arg[1:])
            else:
                getattr(g, op)(*arg)

        r = rall[me]
        q = out_var * narrow(acc[0:24, :] + acc[24:48, :] + acc[48:72, :]) + noise_var * r + beta * gq[before, me]
        p = r + beta * pown[...]
        pown[...] = p
        gq[slot, me] = q
        qown[slot] = q
        share(slot, column_sums(p * q))

        @pl.when(i < CG_STEPS - 1)
        def pass_on():
            gn = Gather(slot, qown.at[slot])
            gn.own()
            for op, *arg in WINDOW:
                if op == "ahead":
                    ahead(ORDER[arg[0]], *arg[1:])
                else:
                    getattr(gn, op)(*arg)

        t = shared(slot)
        alpha = new / spread(t)
        uown[...] += alpha * p
        return alpha, beta, new
    alpha, beta, _ = lax.fori_loop(0, CG_STEPS, step, (zero9 - 1.0, zero9, zero9 + jnp.inf))

    def finish(b, c):
        last_column(b, rall[b, 8], alpha, beta)
        return c
    lax.fori_loop(0, NDEV, finish, 0)

    is_y = lax.broadcasted_iota(jnp.int32, (9, 8, 128), 0) == 8
    u = uown[...]
    z = gq[2, me]
    sol_ref[...] = u
    left = jnp.where(is_y, u, u * (-1.0 / NP))
    own_sum = left * jnp.where(is_y, u, z)
    fit_sum = jnp.where(is_y, u * z, 0.0)
    ai = dot_t(place_ref[3], stack(wide(left))).astype(bf16)
    pp[0:64, 0:ROWS] = ai[0:64]

    def pair_sums(b, carry):
        a_s, a_l = carry
        right = jnp.concatenate([gq[2, b][0:8], uyall[b][None]], axis=0)
        ck = dot_t(stack(wide(right)), place_ref[2]).astype(bf16)
        for h in (0, 1):
            k0 = pl.multiple_of(b * ROWS + h * HALF, HALF)
            s = dot(xk[pl.ds(k0, HALF), :], xi[...])
            g = dot(ck[h * HALF:(h + 1) * HALF, 0:64], pp[0:64, 0:ROWS])
            for r in range(0, HALF, 8):
                sr = jnp.minimum(s[r:r + 8], 0.0)
                t = jnp.exp2(sr) * g[r:r + 8]
                a_s = a_s + t
                a_l = a_l + t * sr
        return a_s, a_l
    zrow = jnp.zeros((8, ROWS), f32)
    a_s, a_l = lax.fori_loop(0, NDEV, pair_sums, (zrow, zrow))

    def total(x):
        return jnp.sum(jnp.sum(x, axis=1, keepdims=True), axis=0, keepdims=True)

    def total5(x):
        return total(sum(x[j] for j in range(9)))
    g_l = out_var * (-LN2) * total(a_l)
    g_s = out_var * total(a_s)
    g_n = noise_var * total5(own_sum)
    fit = 0.5 * total5(fit_sum)
    r24 = lax.broadcasted_iota(jnp.int32, (24, 1), 0)
    share(0, jnp.where(r24 == 0, g_l, jnp.where(r24 == 1, g_s, jnp.where(r24 == 2, g_n, jnp.where(r24 == 3, fit, 0.0)))) / N)
    hyp_ref[...] = jnp.broadcast_to(shared(0)[0:8], (8, 128))


def to_block(main, last):
    m = main.reshape(2, 8, 4, 128).transpose(0, 2, 1, 3).reshape(8, 8, 128)
    return jnp.concatenate([m, jnp.pad(last.reshape(1, 4, 128), ((0, 0), (0, 4), (0, 0)))], axis=0)


def solution(mesh):
    def local(points_own, targets_own, probes_own, log_l, log_s, log_sigma):
        rate = LOG2E * 0.5 * jnp.exp(-2.0 * log_l)
        scal = jnp.stack([jnp.exp(2.0 * log_s), jnp.exp(2.0 * log_sigma), rate])
        scal = jnp.broadcast_to(jnp.pad(scal, (0, 5))[:, None], (8, 128))
        xt = points_own.T
        pay = jnp.stack([to_block(xt[:16], xt[16]), to_block(probes_own.T, targets_own)])
        dma = pltpu.SemaphoreType.DMA
        blocks = pltpu.VMEM((NDEV, 2, 5, 8, 128), f32)
        sol, hyp = pl.pallas_call(
            kernel,
            out_shape=(jax.ShapeDtypeStruct((9, 8, 128), f32), jax.ShapeDtypeStruct((8, 128), f32)),
            in_specs=[pl.BlockSpec(memory_space=pltpu.VMEM)] * 3,
            out_specs=(pl.BlockSpec(memory_space=pltpu.VMEM),) * 2,
            scratch_shapes=[
                pltpu.VMEM((3, NDEV, 9, 8, 128), f32),
                pltpu.VMEM((NDEV, 9, 8, 128), f32),
                pltpu.VMEM((NDEV, 8, 128), f32),
                pltpu.VMEM((NDEV, 8, 128), f32),
                pltpu.VMEM((9, 8, 128), f32),
                pltpu.VMEM((9, 8, 128), f32),
                pltpu.VMEM((N, 128), bf16),
                pltpu.VMEM((128, ROWS), bf16),
                pltpu.VMEM((80, PLANE), bf16),
                pltpu.VMEM((72, ROWS), f32),
                pltpu.VMEM((3, 9, 8, 128), f32),
                pltpu.VMEM((2, 8, 128), f32),
                pltpu.VMEM((2, NDEV, 8, 128), f32),
            ] + [pltpu.VMEM((2, PLANE, HALF), bf16)] * 9 + [
                dma((1,)), dma((3, NDEV)), dma((1,)), dma((2,)),
            ],
            compiler_params=pltpu.CompilerParams(has_side_effects=True, vmem_limit_bytes=67043328),
            name="gp_cg",
        )(pay, scal, jnp.asarray(placements(), bf16))
        v = sol[:8].reshape(2, 4, 8, 128).transpose(1, 3, 0, 2).reshape(ROWS, NP)
        u = sol[8, :4].reshape(ROWS)
        return u, v, hyp[:4, 0]

    return jax.shard_map(
        local,
        mesh=mesh,
        in_specs=(P("dp", None), P("dp"), P("dp", None), P(), P(), P()),
        out_specs=(P("dp"), P("dp", None), P()),
        check_vma=False,
    )
```

time: 4950 us -> 455 us (0.09)
  matrix products: 2070 us -> 0 us
  blocking collectives: 1580 us -> 0 us
  waiting for transfers between devices: 1200 us -> 0 us
  Pallas kernels: 0 us -> 445 us
    dot_general x688 -> x0, matrix products: 2070 us -> none  [the longest x336 1120 us: body(): jnp.dot(kernel, col_right, precision=lax.Precision.HIGHEST, preferred_ele...]
    psum x40 -> x0, blocking collectives: 1580 us -> none  [the longest x19 757 us: local(): new_norm = lax.psum(jnp.sum(residual * residual, axis=0), 'dp')]
    all_gather x22 -> x0, waiting for transfers between devices: 1200 us -> none  [the longest x20 1090 us: apply_kernel(): search_all = lax.all_gather(search_own, 'dp', tiled=True)]
    pallas_call x0 -> x1, Pallas kernels: none -> 445 us  [local(): pl.pallas_call(kernel, out_shape=(jax.ShapeDtypeStruct((9, 8, 128), f32),...]
  transfers between devices with their start and end apart: 22 -> 0, of which waited for: 22 -> 0; matrix products, arithmetic and copies ran while one was open for 0% -> 0% of each run, Pallas kernels for 0% -> 0%
where the time goes in v3:
time: 455 us
  Pallas kernels  445 us (98%)
  local copies, waits for them, and re-layouts  6.09 us (1%)
    pallas_call x1, Pallas kernels, local(): pl.pallas_call(kernel, out_shape=(jax.ShapeDtypeStruct((9, 8, 128), f32),...  445 us

profile of v3, /device:TPU:0, one launch (start us, length us, event | category | flops | bytes accessed | tf_op | source)
XLA Modules:
  0.0 454.8 jit_solution(12885203581457235100)
XLA Ops:
  0.6 0.0 copy-start
  0.6 0.8 slice.20
  1.4 0.7 slice.21
  2.1 0.0 copy-start.1
  2.1 0.0 copy-done
  2.1 0.7 copy-done.1
  2.8 0.6 pad_maximum_fusion.pay_ref
  5.5 0.1 select_maximum_fusion.2
  5.6 0.7 broadcast_in_dim.2.scal_ref
  6.3 445.3 %gp_cg.1 = (f32[9,8,128]{2,1,0:T(8,128)}, f32[8,128]{1,0:T(8,128)}) custom-call(f32[2,9,8,128]{3,2,1,0:T(8,128)} %pad_maximum_fusion.pay_ref, f32[8,128]{1,0:T(8,128)} %broadcast_in_dim.2.scal_ref, bf16[4,72,128]{2,1,0:T(8,128)(2,1)} %constant.11.clone.place_ref), custom_call_target="tpu_custom_call" | custom-call | tf_op jit(solution)/shard_map/gp_cg/pallas_call | solution.py:397
  451.5 1.4 slice.18
  452.9 0.0 copy-start.2
  452.9 1.2 slice_bitcast_fusion
  454.2 0.0 copy-done.2
  454.2 0.6 slice_reduce_fusion
  (1 shorter events, 0.0 us)
Async XLA Ops:
  0.6 1.5 copy-start
  2.1 0.7 copy-start.1
  452.9 1.3 copy-start.2
